TPU v7x, 32 devices: a whole 2x2x4 slice. The times are simulated.
32 devices in a mesh: patch: 8 (over z, y), sub: 4 (over x, core).
Axes of the slice: x: 2, y: 2, z: 4, core: 2. Of those that a mesh axis runs over, the one named last changes fastest.
Arguments:
- heat: float32 [262144], P(('patch', 'sub')), may hold values from -6 to 6
- basis: bfloat16 [9, 524288], P(None, ('patch', 'sub')), may hold values from -3 to 3
- area: float32 [524288], P(('patch', 'sub')), may hold values from 0.2 to 2
- corners: int32 [3, 524288], P(None, ('patch', 'sub')), may hold values from 0 to 9215, as said below
- send_sub: int32 [4096], P(('patch', 'sub')), may hold values from 0 to 8191
- send_pat: int32 [4, 4096], P(None, ('patch', 'sub')), may hold values from 0 to 8191
- live_faces: int32 [32], P(('patch', 'sub')), may hold values from 12288 to 16384, as said below
Outputs:
- divergence: float32 [262144], P(('patch', 'sub'))
Inputs may be any that keep to these rules, and one draw needn't show every extreme that they name: Face slot f of a device lies in tile t = f // 128; each of its corners is either an owned position in [64 t - 128, 64 t + 128) or a remote position from 8192 + 256 (t mod (4)) up to 255 beyond that; every position of the device's table is read by some face of the device. `live_faces`: some device has all 16384 slots live.
All inputs are finite; a program needn't handle non-finite values.
Results may differ from a plain program's by a relative error of at most 0.0003.
Values sent between devices are 32-bit elements; how exact they have to be, the bound alone decides.
A program may use at most 64 MiB of HBM per device.

v0:
```python
import jax
import jax.numpy as jnp
from jax import lax
from jax.sharding import PartitionSpec as P

RADIUS = 2


def from_behind(x, axis, by):
    length = lax.axis_size(axis)
    return lax.ppermute(x, axis, [(i, (i + by) % length) for i in range(length)])


def offset_list():
    return [k + 1 for k in range(RADIUS)] + [-(k + 1) for k in range(RADIUS)]


def tile_terms(
    window,
    remote_window,
    corner_tile,
    basis_tile,
    area_tile,
    start,
    remote_start,
    first_slot,
    live_count,
):
    window_pos = jnp.arange(window.shape[0])
    remote_pos = jnp.arange(remote_window.shape[0])
    onehot_near = (corner_tile[:, :, None] - start == window_pos).astype(jnp.float32)
    onehot_far = (corner_tile[:, :, None] - remote_start == remote_pos).astype(jnp.float32)
    values = jnp.einsum("kfw,w->kf", onehot_near, window, precision=lax.Precision.HIGHEST)
    values = values + jnp.einsum(
        "kfw,w->kf", onehot_far, remote_window, precision=lax.Precision.HIGHEST
    )
    width = corner_tile.shape[1]
    gradients = basis_tile.astype(jnp.float32).reshape(3, 3, width)
    gradient = jnp.sum(gradients * values[:, None, :], axis=0)
    length = jnp.sqrt(jnp.sum(gradient * gradient, axis=0))
    field = -gradient / jnp.maximum(length, 1.0)
    projected = jnp.sum(gradients * field[None, :, :], axis=1)
    live_mask = first_slot + jnp.arange(width) < live_count
    weight = jnp.where(live_mask, area_tile, 0.0)
    terms = projected * weight[None, :]
    near_sums = jnp.einsum("kfw,kf->w", onehot_near, terms, precision=lax.Precision.HIGHEST)
    far_sums = jnp.einsum("kfw,kf->w", onehot_far, terms, precision=lax.Precision.HIGHEST)
    return (near_sums, far_sums)


def face_terms(heat, remote, corners, basis, area, live_count):
    owned = heat.shape[0]
    slots = corners.shape[1]
    tiles = slots // 128
    remote_len = remote.shape[0]
    remote_win = min(256, remote_len)
    remote_blocks = remote_len // remote_win
    padded = jnp.pad(heat, (128, 128))
    pieces = padded.reshape(tiles + 4, 64)
    windows = jnp.concatenate([pieces[shift : shift + tiles] for shift in range(4)], axis=1)
    remote_tiles = jnp.tile(remote.reshape(remote_blocks, remote_win), (tiles // remote_blocks, 1))
    tile_ids = jnp.arange(tiles)
    starts = 64 * tile_ids - 128
    remote_starts = owned + remote_win * (tile_ids % remote_blocks)
    first_slots = 128 * tile_ids
    corner_tiles = corners.reshape(3, tiles, 128).transpose(1, 0, 2)
    basis_tiles = basis.reshape(9, tiles, 128).transpose(1, 0, 2)
    area_tiles = area.reshape(tiles, 128)
    batch = 1
    limit = max(1, tiles // 16)
    while batch * 2 <= limit and tiles % (batch * 2) == 0:
        batch = batch * 2
    groups = tiles // batch
    packed = (
        windows,
        remote_tiles,
        corner_tiles,
        basis_tiles,
        area_tiles,
        starts,
        remote_starts,
        first_slots,
    )
    packed = jax.tree.map(lambda array: array.reshape((groups, batch) + array.shape[1:]), packed)

    def run_group(pack):
        return jax.vmap(
            lambda w, r, c, b, a, s, q, f: tile_terms(w, r, c, b, a, s, q, f, live_count)
        )(*pack)

    near_sums, far_sums = lax.map(run_group, packed)
    near_sums = near_sums.reshape(tiles, 4, 64)
    summed = jnp.zeros((tiles + 4, 64), jnp.float32)
    for shift in range(4):
        summed = summed + jnp.pad(near_sums[:, shift], ((shift, 4 - shift), (0, 0)))
    owned_sums = summed.reshape(-1)[128 : 128 + owned]
    far_sums = far_sums.reshape(tiles // remote_blocks, remote_blocks, remote_win)
    remote_sums = jnp.sum(far_sums, axis=0).reshape(-1)
    return (owned_sums, remote_sums)


def per_device(heat, basis, area, corners, send_sub, send_pat, live_faces):
    sub_count = lax.axis_size("sub")
    group_size = send_sub.shape[0]
    block_size = send_pat.shape[1]
    offsets = offset_list()
    group_send = jnp.take(heat, send_sub)
    group_values = lax.all_gather(group_send, "sub", axis=0, tiled=True)
    outgoing = jnp.take(heat, send_pat)
    incoming = jnp.stack(
        [
            from_behind(outgoing[block_index], "patch", offset)
            for block_index, offset in enumerate(offsets)
        ]
    )
    remote = jnp.concatenate([group_values, incoming.reshape(-1)])
    result, remote_sums = face_terms(heat, remote, corners, basis, area, live_faces[0])
    group_part = remote_sums[: sub_count * group_size]
    patch_part = remote_sums[sub_count * group_size :].reshape(2 * RADIUS, block_size)
    group_back = lax.psum_scatter(group_part, "sub", scatter_dimension=0, tiled=True)
    returned = jnp.stack(
        [
            from_behind(patch_part[block_index], "patch", -offset)
            for block_index, offset in enumerate(offsets)
        ]
    )
    result = result.at[send_sub].add(group_back)
    result = result.at[send_pat.reshape(-1)].add(returned.reshape(-1))
    return result


def solution(mesh):
    placed = (
        P(("patch", "sub")),
        P(None, ("patch", "sub")),
        P(("patch", "sub")),
        P(None, ("patch", "sub")),
        P(("patch", "sub")),
        P(None, ("patch", "sub")),
        P(("patch", "sub")),
    )
    return jax.shard_map(
        per_device, mesh=mesh, in_specs=placed, out_specs=P(("patch", "sub")), check_vma=False
    )
```

profile of v0, /device:TPU:0, one launch (start us, length us, event | category | flops | bytes accessed | tf_op | source)
XLA Modules:
  0.0 180.9 jit_solution(4505595029857006863)
XLA Ops:
  0.7 3.5 %gather_fusion.1 = f32[512]{0:T(512)S(1)} fusion(f32[8192]{0:T(1024)} %param.9, s32[1024]{0:T(1024)S(1)} %pad_clamp_fusion), kind=kCustom, calls=%fused_computation.1 | custom fusion | bytes 6144 | tf_op jit(solution)/shard_map/jit(_take)/gather | solution.py:109
  4.2 3.0 %collective-permute-start = (f32[128]{0:T(128)S(1)}, f32[128]{0:T(128)S(1)}, u32[]{:S(2)}, u32[]{:S(2)}) collective-permute-start(f32[128]{0:T(128)S(1)} %get-tuple-element.135), channel_id=1, source_target_pairs={{0,4},{4,8},{8,12},{12,16},{16,20},{20,24},{24,28},{28,0},{1,5},{5... | collective-permute-start | bytes 1544 | tf_op jit(solution)/shard_map/ppermute | solution.py:11
  7.3 1.6 collective-permute-start.1
  8.9 3.2 %collective-permute-start.2 = (f32[128]{0:T(128)S(1)}, f32[128]{0:T(128)S(1)}, u32[]{:S(2)}, u32[]{:S(2)}) collective-permute-start(f32[128]{0:T(128)S(1)} %get-tuple-element.137), channel_id=1, source_target_pairs={{0,28},{4,0},{8,4},{12,8},{16,12},{20,16},{24,20},{28,24},{1,29},{... | collective-permute-start | bytes 1544 | tf_op jit(solution)/shard_map/ppermute | solution.py:11
  13.9 5.1 %all-gather = f32[4,1,128]{2,1,0:T(1,128)S(1)} all-gather(f32[1,1,128]{2,1,0:T(1,128)S(1)} %fusion.22), channel_id=1, replica_groups=mesh['patch'=8,'sub'=4] {'sub'}, dimensions={0}, use_global_device_ids=true | all-gather | bytes 2560 | tf_op jit(solution)/shard_map/all_gather | solution.py:108
  22.6 140.8 %while.12 = (s32[]{:T(128)}, f32[16,8,256]{2,1,0:T(8,128)S(1)}, f32[16,8,256]{2,1,0:T(8,128)S(1)}, s32[16,8,3,128]{3,2,1,0:T(4,128)}, s32[16,8]{1,0:T(8,128)S(1)...) while((s32[]{:T(128)}, f32[16,8,256]{2,1,0:T(8,128)S(1)}, ...), condition=%wide.region_4.5_spmd, body=%wide.region_0.4_spmd.sunk | while | flops 40971264 | bytes 483781 | solution.py:91
  23.5 1.7 fusion.44
  25.2 1.7 fusion.45
  28.4 1.5 fusion.50
  29.9 1.5 fusion.49
  32.3 1.7 fusion.44
  34.0 1.7 fusion.45
  37.2 1.5 fusion.50
  38.7 1.5 fusion.49
  41.1 1.7 fusion.44
  42.8 1.7 fusion.45
  46.0 1.5 fusion.50
  47.5 1.5 fusion.49
  49.9 1.7 fusion.44
  51.6 1.7 fusion.45
  54.8 1.5 fusion.50
  56.3 1.5 fusion.49
  58.7 1.7 fusion.44
  60.4 1.7 fusion.45
  63.6 1.5 fusion.50
  65.1 1.5 fusion.49
  67.5 1.7 fusion.44
  69.2 1.7 fusion.45
  72.4 1.5 fusion.50
  73.9 1.5 fusion.49
  76.3 1.7 fusion.44
  78.0 1.7 fusion.45
  82.7 1.5 fusion.49
  85.1 1.7 fusion.44
  86.8 1.7 fusion.45
  91.5 1.5 fusion.49
  93.9 1.7 fusion.44
  95.6 1.7 fusion.45
  100.3 1.5 fusion.49
  102.7 1.7 fusion.44
  104.4 1.7 fusion.45
  109.1 1.5 fusion.49
  111.5 1.7 fusion.44
  113.2 1.7 fusion.45
  117.9 1.5 fusion.49
  120.3 1.7 fusion.44
  122.0 1.7 fusion.45
  126.7 1.5 fusion.49
  129.1 1.7 fusion.44
  130.8 1.7 fusion.45
  135.5 1.5 fusion.49
  137.9 1.7 fusion.44
  139.6 1.7 fusion.45
  144.3 1.5 fusion.49
  146.7 1.7 fusion.44
  148.4 1.7 fusion.45
  153.1 1.5 fusion.49
  155.5 1.7 fusion.44
  157.2 1.7 fusion.45
  161.9 1.5 fusion.49
  163.9 2.0 %collective-permute-start.4 = (f32[128]{0:T(128)S(1)}, f32[128]{0:T(128)S(1)}, u32[]{:S(2)}, u32[]{:S(2)}) collective-permute-start(f32[128]{0:T(128)S(1)} %get-tuple-element.131), channel_id=1, source_target_pairs={{0,28},{4,0},{8,4},{12,8},{16,12},{20,16},{24,20},{28,24},{1,29},{... | collective-permute-start | bytes 1544 | tf_op jit(solution)/shard_map/ppermute | solution.py:11
  166.4 1.5 collective-permute-start.6
  168.1 6.5 %all-reduce.5 = f32[512]{0:T(512)S(1)} all-reduce(f32[512]{0:T(512)S(1)} %bitcast.134), channel_id=2, replica_groups=mesh['patch'=8,'sub'=4] {'sub'}, use_global_device_ids=true, to_apply=%region_6.7.clone | all-reduce | flops 512 | bytes 4096
  176.6 4.4 %scatter_fusion.1 = f32[8192]{0:T(1024)} fusion(f32[8192]{0:T(1024)} %copy-done.1, s32[512]{0:T(512)S(1)} %bitcast.133, f32[512]{0:T(512)S(1)} %maximum_bitcast_fusion), kind=kCustom, calls=%fused_computation.3 | custom fusion | flops 512 | bytes 8192 | tf_op jit(solution)/shard_map/scatter-add | solution.py:128
  (332 shorter events, 60.4 us)
Async XLA Ops:
  0.7 3.5 %copy-start.3 = (s32[4,128]{1,0:T(4,128)S(1)}, s32[4,128]{1,0:T(4,128)}, u32[]{:S(2)}) copy-start(s32[4,128]{1,0:T(4,128)} %param.14) | copy-start | bytes 6148
  0.7 11.7 %copy-start = (f32[8192]{0:T(1024)S(1)}, f32[8192]{0:T(1024)}, u32[]{:S(2)}) copy-start(f32[8192]{0:T(1024)} %param.9) | copy-start | bytes 98308
  0.7 11.9 %copy-start.4 = (s32[128]{0:T(128)S(1)}, s32[128]{0:T(128)}, u32[]{:S(2)}) copy-start(s32[128]{0:T(128)} %param.13) | copy-start | bytes 1540
  4.2 18.2 %collective-permute-start = (f32[128]{0:T(128)S(1)}, f32[128]{0:T(128)S(1)}, u32[]{:S(2)}, u32[]{:S(2)}) collective-permute-start(f32[128]{0:T(128)S(1)} %get-tuple-element.135), channel_id=1, source_target_pairs={{0,4},{4,8},{8,12},{12,16},{16,20},{20,24},{24,28},{28,0},{1,5},{5... | collective-permute-start | bytes 1544 | tf_op jit(solution)/shard_map/ppermute | solution.py:11
  7.3 15.2 %collective-permute-start.1 = (f32[128]{0:T(128)S(1)}, f32[128]{0:T(128)S(1)}, u32[]{:S(2)}, u32[]{:S(2)}) collective-permute-start(f32[128]{0:T(128)S(1)} %get-tuple-element.138), channel_id=1, source_target_pairs={{0,8},{4,12},{8,16},{12,20},{16,24},{20,28},{24,0},{28,4},{1,9},{5... | collective-permute-start | bytes 1544 | tf_op jit(solution)/shard_map/ppermute | solution.py:11
  8.9 13.6 %collective-permute-start.2 = (f32[128]{0:T(128)S(1)}, f32[128]{0:T(128)S(1)}, u32[]{:S(2)}, u32[]{:S(2)}) collective-permute-start(f32[128]{0:T(128)S(1)} %get-tuple-element.137), channel_id=1, source_target_pairs={{0,28},{4,0},{8,4},{12,8},{16,12},{20,16},{24,20},{28,24},{1,29},{... | collective-permute-start | bytes 1544 | tf_op jit(solution)/shard_map/ppermute | solution.py:11
  12.1 10.4 %collective-permute-start.3 = (f32[128]{0:T(128)S(1)}, f32[128]{0:T(128)S(1)}, u32[]{:S(2)}, u32[]{:S(2)}) collective-permute-start(f32[128]{0:T(128)S(1)} %get-tuple-element.136), channel_id=1, source_target_pairs={{0,24},{4,28},{8,0},{12,4},{16,8},{20,12},{24,16},{28,20},{1,25},{... | collective-permute-start | bytes 1544 | tf_op jit(solution)/shard_map/ppermute | solution.py:11
  12.5 7.8 %copy-start.2 = (bf16[9,16384]{1,0:T(8,128)(2,1)S(1)}, bf16[9,16384]{1,0:T(8,128)(2,1)}, u32[]{:S(2)}) copy-start(bf16[9,16384]{1,0:T(8,128)(2,1)} %param.10) | copy-start | bytes 884740
  20.4 0.7 copy-start.5
  163.9 12.1 %collective-permute-start.4 = (f32[128]{0:T(128)S(1)}, f32[128]{0:T(128)S(1)}, u32[]{:S(2)}, u32[]{:S(2)}) collective-permute-start(f32[128]{0:T(128)S(1)} %get-tuple-element.131), channel_id=1, source_target_pairs={{0,28},{4,0},{8,4},{12,8},{16,12},{20,16},{24,20},{28,24},{1,29},{... | collective-permute-start | bytes 1544 | tf_op jit(solution)/shard_map/ppermute | solution.py:11
  165.9 10.1 %collective-permute-start.5 = (f32[128]{0:T(128)S(1)}, f32[128]{0:T(128)S(1)}, u32[]{:S(2)}, u32[]{:S(2)}) collective-permute-start(f32[128]{0:T(128)S(1)} %get-tuple-element.134), channel_id=1, source_target_pairs={{0,24},{4,28},{8,0},{12,4},{16,8},{20,12},{24,16},{28,20},{1,25},{... | collective-permute-start | bytes 1544 | tf_op jit(solution)/shard_map/ppermute | solution.py:11
  166.4 9.6 %collective-permute-start.6 = (f32[128]{0:T(128)S(1)}, f32[128]{0:T(128)S(1)}, u32[]{:S(2)}, u32[]{:S(2)}) collective-permute-start(f32[128]{0:T(128)S(1)} %get-tuple-element.133), channel_id=1, source_target_pairs={{0,4},{4,8},{8,12},{12,16},{16,20},{20,24},{24,28},{28,0},{1,5},{5... | collective-permute-start | bytes 1544 | tf_op jit(solution)/shard_map/ppermute | solution.py:11
  167.9 8.1 %collective-permute-start.7 = (f32[128]{0:T(128)S(1)}, f32[128]{0:T(128)S(1)}, u32[]{:S(2)}, u32[]{:S(2)}) collective-permute-start(f32[128]{0:T(128)S(1)} %get-tuple-element.132), channel_id=1, source_target_pairs={{0,8},{4,12},{8,16},{12,20},{16,24},{20,28},{24,0},{28,4},{1,9},{5... | collective-permute-start | bytes 1544 | tf_op jit(solution)/shard_map/ppermute | solution.py:11
  176.0 0.6 copy-start.1
where the time goes:
time: 183 us; the launch traced here: 181 us
  matrix products  102 us (56%)
  other arithmetic  43.4 us (24%)
  starting transfers between devices  12.3 us (7%)
  blocking collectives  11.5 us (6%)
  local copies, waits for them, and re-layouts  9.11 us (5%)
  loops' own time  1.96 us (1%)
    dot_general x16, matrix products, tile_terms(): jnp.einsum('kfw,w->kf', onehot_far, remote_window, precision=lax.Precisio...  27.1 us
    dot_general x16, matrix products, tile_terms(): jnp.einsum('kfw,w->kf', onehot_near, window, precision=lax.Precision.HIGH...  27 us
    dot_general x16, matrix products, tile_terms(): jnp.einsum('kfw,kf->w', onehot_far, terms, precision=lax.Precision.HIGHEST)  23.9 us
    dot_general x16, matrix products, tile_terms(): jnp.einsum('kfw,kf->w', onehot_near, terms, precision=lax.Precision.HIGHEST)  23.6 us
    select_n x16, other arithmetic, tile_terms(): weight = jnp.where(live_mask, area_tile, 0.0)  22.5 us
    sub x16, other arithmetic, tile_terms(): corner_tile[:, :, None] - remote_start == remote_pos  12.8 us
    ppermute x8, starting transfers between devices, from_behind(): lax.ppermute(x, axis, [(i, (i + by) % length) for i in range(length)])  12.3 us
    unnamed x1, blocking collectives  6.48 us
  transfers between devices with their start and end apart: 8, of which 0 were waited for; matrix products, arithmetic and copies ran while one was open for 3% of the time, Pallas kernels for 0%

commit v1 on v0

v1 whole, which is shorter than its diff:
```python
import functools

import jax
import jax.numpy as jnp
from jax import lax
from jax.experimental import pallas as pl
from jax.experimental.pallas import tpu as pltpu
from jax.sharding import PartitionSpec as P

RADIUS = 2
LANES = 128
F32 = jnp.float32
BF16 = jnp.bfloat16


def offset_list():
    return [k + 1 for k in range(RADIUS)] + [-(k + 1) for k in range(RADIUS)]


def lane_pick(rows, lanes):
    return jnp.take_along_axis(rows, lanes, axis=1, mode="promise_in_bounds")


def split_two(x):
    high = x.astype(BF16).astype(F32)
    return high, x - high


def wide(row, count):
    return jnp.broadcast_to(row, (count, row.shape[1]))


def rows_dot(a, b):
    return lax.dot_general(a, b, (((1,), (1,)), ((), ())), preferred_element_type=F32)


def kernel(
    patch_count,
    sub_count,
    share,
    heat_ref,
    sends_ref,
    live_ref,
    basis_hbm,
    area_hbm,
    corners_hbm,
    out_ref,
    basis_in,
    area_in,
    corners_in,
    in_sem,
    padded,
    main,
    other,
    flat,
    grads,
    near_val,
    spot,
    parts,
    far,
    near_sum,
    send_group,
    send_patch,
    recv_group,
    recv_patch,
    back_group,
    back_patch,
    home_group,
    home_patch,
    sems_group,
    sems_patch,
    home_sems_group,
    home_sems_patch,
):
    p = lax.axis_index("patch")
    s = lax.axis_index("sub")
    offsets = offset_list()
    blocks = len(offsets)
    own_rows = heat_ref.shape[0]
    tiles = area_in.shape[0]
    groups = tiles // 8
    far_rows = far.shape[0]
    per_row = LANES // share
    group_rows = sub_count // per_row

    copies = [
        pltpu.make_async_copy(corners_hbm, corners_in, in_sem.at[0]),
        pltpu.make_async_copy(basis_hbm, basis_in, in_sem.at[1]),
        pltpu.make_async_copy(area_hbm, area_in, in_sem.at[2]),
    ]
    for copy in copies:
        copy.start()

    subs = [lax.rem(s + d, sub_count) for d in range(1, sub_count)]
    behind = [lax.rem(s + sub_count - d, sub_count) for d in range(1, sub_count)]
    ahead_patch = [lax.rem(p + o + patch_count, patch_count) for o in offsets]
    back_to = [lax.rem(p - o + patch_count, patch_count) for o in offsets]
    barrier = pltpu.get_barrier_semaphore()
    for target in subs:
        pl.semaphore_signal(barrier, inc=1, device_id={"patch": p, "sub": target})
    for target in ahead_patch:
        pl.semaphore_signal(barrier, inc=1, device_id={"patch": target, "sub": s})

    heat = heat_ref[...]
    piece_a, rest = split_two(heat)
    piece_b, piece_c = split_two(rest)
    pieces = jnp.concatenate([piece_a, piece_b, piece_c], axis=0).astype(BF16)
    lists = sends_ref[...]
    rows_of = lax.shift_right_logical(lists, 7).astype(F32)
    lanes_of = (lists & (LANES - 1)).astype(F32)
    row_iota = lax.broadcasted_iota(jnp.int32, (own_rows, LANES), 0).astype(F32)
    lane_iota = lax.broadcasted_iota(jnp.int32, (LANES, LANES), 0).astype(F32)
    for b in range(1 + blocks):
        hit = jnp.where(wide(rows_of[b : b + 1], own_rows) == row_iota, 1.0, 0.0)
        hit = jnp.concatenate([hit, hit, hit], axis=0).astype(BF16)
        table = lax.dot_general(
            pieces, hit, (((0,), (0,)), ((), ())), preferred_element_type=F32
        )
        picked = jnp.where(wide(lanes_of[b : b + 1], LANES) == lane_iota, table, 0.0)
        row = jnp.sum(picked, axis=0, keepdims=True)
        if b == 0:
            send_group[0] = row
        else:
            send_patch[b - 1] = row

    pl.semaphore_wait(barrier, sub_count - 1 + blocks)

    def to_sub(src, dst, send, recv, target):
        return pltpu.make_async_remote_copy(
            src_ref=src,
            dst_ref=dst,
            send_sem=send,
            recv_sem=recv,
            device_id={"patch": p, "sub": target},
        )

    def to_patch(src, dst, send, recv, target):
        return pltpu.make_async_remote_copy(
            src_ref=src,
            dst_ref=dst,
            send_sem=send,
            recv_sem=recv,
            device_id={"patch": target, "sub": s},
        )

    sent = []
    for j in range(blocks):
        copy = to_patch(
            send_patch.at[j],
            recv_patch.at[j],
            sems_patch.at[0, j],
            sems_patch.at[1, j],
            ahead_patch[j],
        )
        copy.start()
        sent.append(copy)
    for d, target in enumerate(subs):
        copy = to_sub(
            send_group.at[0],
            recv_group.at[s],
            sems_group.at[0, d],
            sems_group.at[1, s],
            target,
        )
        copy.start()
        sent.append(copy)

    lane8 = lax.broadcasted_iota(jnp.int32, (own_rows, LANES), 1)
    padded[...] = jnp.zeros_like(padded)
    padded[8 : 8 + own_rows] = heat
    before = padded[7 : 7 + own_rows]
    after = padded[9 : 9 + own_rows]
    main[pl.ds(0, own_rows, stride=2), :] = heat
    main[pl.ds(1, own_rows, stride=2), :] = heat
    other[pl.ds(0, own_rows, stride=2), :] = before
    other[pl.ds(1, own_rows, stride=2), :] = jnp.where(lane8 < LANES // 2, after, before)

    for copy in copies:
        copy.wait()
    sub8 = lax.broadcasted_iota(jnp.int32, (8, LANES), 0)

    def prepare(g, carry):
        first = pl.multiple_of(8 * g, 8)
        for i in range(8):
            cols = pl.ds(pl.multiple_of((first + i) * LANES, LANES), LANES)
            flat[16 * i : 16 * i + 9, :] = basis_in[:, cols].astype(F32)
            spot[16 * i : 16 * i + 3, :] = corners_in[:, cols]
        for r in range(9):
            grads[r, pl.ds(first, 8), :] = flat[pl.ds(r, 8, stride=16), :]
        mains = main[pl.ds(first, 8), :]
        others = other[pl.ds(first, 8), :]
        home = lax.shift_right_logical(first + sub8, 1)
        for k in range(3):
            pos = spot[pl.ds(k, 8, stride=16), :]
            lanes = pos & (LANES - 1)
            rows = lax.shift_right_logical(pos, 7)
            near_val[k, pl.ds(first, 8), :] = jnp.where(
                rows == home, lane_pick(mains, lanes), lane_pick(others, lanes)
            )
            parts[k, pl.ds(first, 8), :] = pos
        return carry

    lax.fori_loop(0, groups, prepare, 0)

    for d, source in enumerate(behind):
        to_sub(
            send_group.at[0],
            recv_group.at[source],
            sems_group.at[0, d],
            sems_group.at[1, source],
            source,
        ).wait_recv()
    for j in range(blocks):
        to_patch(
            send_patch.at[j],
            recv_patch.at[j],
            sems_patch.at[0, j],
            sems_patch.at[1, j],
            ahead_patch[j],
        ).wait_recv()
    recv_group[s] = send_group[0]
    lane1 = lax.broadcasted_iota(jnp.int32, (1, LANES), 1)
    for r in range(group_rows):
        row = recv_group[r * per_row]
        for q in range(1, per_row):
            moved = pltpu.roll(recv_group[r * per_row + q], q * share, 1)
            row = jnp.where(lane1 < q * share, row, moved)
        far[r : r + 1, :] = row
    for j in range(blocks):
        far[group_rows + j : group_rows + j + 1, :] = recv_patch[j]

    window_rows = 2
    windows = far_rows // window_rows
    even = jnp.concatenate([far[pl.ds(0, windows, stride=2), :]] * (8 // windows), axis=0)
    odd = jnp.concatenate([far[pl.ds(1, windows, stride=2), :]] * (8 // windows), axis=0)
    live = live_ref[0]
    lane_ids = lax.broadcasted_iota(jnp.int32, (8, LANES), 1)
    id_iota = lax.broadcasted_iota(jnp.int32, (16, LANES), 0).astype(F32).astype(BF16)
    hot_iota = lane_iota.astype(BF16)
    one = jnp.ones((16, LANES), BF16)
    zero = jnp.zeros((16, LANES), BF16)
    near_sum[...] = jnp.zeros_like(near_sum)

    def work(g, far_acc):
        first = pl.multiple_of(8 * g, 8)
        tile = pl.ds(first, 8)
        values, lanes, ids = [], [], []
        for k in range(3):
            pos = parts[k, tile, :]
            lane = pos & (LANES - 1)
            row = lax.shift_right_logical(pos, 7)
            remote = jnp.where((row & 1) == 0, lane_pick(even, lane), lane_pick(odd, lane))
            values.append(jnp.where(row >= own_rows, remote, near_val[k, tile, :]))
            lanes.append(lane.astype(F32))
            ids.append(
                jnp.where(row >= own_rows, row - own_rows, row - 4 * g + 1 + far_rows).astype(F32)
            )
        grad = [[grads[3 * k + c, tile, :] for c in range(3)] for k in range(3)]
        total = [sum(grad[k][c] * values[k] for k in range(3)) for c in range(3)]
        squared = total[0] * total[0] + total[1] * total[1] + total[2] * total[2]
        scale = -1.0 / jnp.maximum(jnp.sqrt(squared), 1.0)
        slot = (first + sub8) * LANES + lane_ids
        scale = scale * jnp.where(slot < live, area_in[tile, :], 0.0)
        tops, lows = [], []
        for k in range(3):
            term = (
                grad[k][0] * total[0] + grad[k][1] * total[1] + grad[k][2] * total[2]
            ) * scale
            high, low = split_two(term)
            tops.append(high)
            lows.append(low)
        acc = jnp.zeros((32, LANES), F32)
        for pair in range(4):
            left, right = [], []
            for i in (2 * pair, 2 * pair + 1):
                for k in range(3):
                    id_wide = wide(ids[k][i : i + 1], 16).astype(BF16)
                    top = wide(tops[k][i : i + 1], 16).astype(BF16)
                    low = wide(lows[k][i : i + 1], 16).astype(BF16)
                    mask = id_wide == id_iota
                    left.append(
                        jnp.concatenate([jnp.where(mask, top, zero), jnp.where(mask, low, zero)], axis=0)
                    )
                    lane_wide = wide(lanes[k][i : i + 1], 16).astype(BF16)
                    right.append(
                        jnp.concatenate(
                            [
                                jnp.where(lane_wide == hot_iota[16 * n : 16 * n + 16], one, zero)
                                for n in range(LANES // 16)
                            ],
                            axis=0,
                        )
                    )
            acc = acc + rows_dot(jnp.concatenate(left, axis=1), jnp.concatenate(right, axis=1))
        acc = acc[:16] + acc[16:]
        at = pl.ds(pl.multiple_of(4 * g, 4), 8)
        near_sum[at, :] = near_sum[at, :] + acc[8:]
        return far_acc + acc[:8]

    sums = lax.fori_loop(0, groups, work, jnp.zeros((8, LANES), F32))

    for target in range(sub_count):
        row = sums[target // per_row : target // per_row + 1]
        if per_row > 1:
            shift = (target % per_row) * share
            if shift:
                row = pltpu.roll(row, LANES - shift, 1)
            row = jnp.where(lane1 < share, row, 0.0)
        back_group[target] = row
    for j in range(blocks):
        back_patch[j] = sums[group_rows + j : group_rows + j + 1]
    for j in range(blocks):
        copy = to_patch(
            back_patch.at[j],
            home_patch.at[j],
            home_sems_patch.at[0, j],
            home_sems_patch.at[1, j],
            back_to[j],
        )
        copy.start()
        sent.append(copy)
    for d, target in enumerate(subs):
        copy = to_sub(
            back_group.at[target],
            home_group.at[s],
            home_sems_group.at[0, d],
            home_sems_group.at[1, s],
            target,
        )
        copy.start()
        sent.append(copy)
    hot = []
    for b in range(1 + blocks):
        lane_wide = wide(lanes_of[b : b + 1], LANES)
        hot.append(jnp.where(lane_wide == lane_iota, 1.0, 0.0).astype(BF16))
    hot = jnp.concatenate(hot, axis=1)

    for d, source in enumerate(behind):
        to_sub(
            back_group.at[source],
            home_group.at[source],
            home_sems_group.at[0, d],
            home_sems_group.at[1, source],
            source,
        ).wait_recv()
    for j in range(blocks):
        to_patch(
            back_patch.at[j],
            home_patch.at[j],
            home_sems_patch.at[0, j],
            home_sems_patch.at[1, j],
            back_to[j],
        ).wait_recv()
    total = back_group[s]
    for source in behind:
        total = total + home_group[source]
    returned = [total] + [home_patch[j] for j in range(blocks)]
    left = []
    for b in range(1 + blocks):
        hit = wide(rows_of[b : b + 1], own_rows) == row_iota
        high, low = split_two(returned[b])
        left.append(
            jnp.concatenate(
                [
                    jnp.where(hit, wide(high, own_rows), 0.0),
                    jnp.where(hit, wide(low, own_rows), 0.0),
                ],
                axis=0,
            ).astype(BF16)
        )
    added = rows_dot(jnp.concatenate(left, axis=1), hot)
    out_ref[...] = near_sum[1 : 1 + own_rows, :] + added[:own_rows] + added[own_rows:]
    for copy in sent:
        copy.wait_send()


def solution(mesh):
    patch_count, sub_count = mesh.shape["patch"], mesh.shape["sub"]

    def per_device(heat, basis, area, corners, send_sub, send_pat, live_faces):
        owned, slots = heat.shape[0], area.shape[0]
        share = send_sub.shape[0]
        blocks, block_size = send_pat.shape
        own_rows, tiles = owned // LANES, slots // LANES
        far_rows = (sub_count * share + blocks * block_size) // LANES
        assert block_size == LANES and LANES % share == 0 and far_rows == 8
        lists = jnp.concatenate([jnp.pad(send_sub, (0, LANES - share))[None], send_pat], axis=0)
        vmem = pl.BlockSpec(memory_space=pltpu.VMEM)
        hbm = pl.BlockSpec(memory_space=pl.ANY)
        row = (1, LANES)
        out = pl.pallas_call(
            functools.partial(kernel, patch_count, sub_count, share),
            out_shape=jax.ShapeDtypeStruct((own_rows, LANES), F32),
            in_specs=[vmem, vmem, pl.BlockSpec(memory_space=pltpu.SMEM), hbm, hbm, hbm],
            out_specs=vmem,
            scratch_shapes=[
                pltpu.VMEM(basis.shape, basis.dtype),
                pltpu.VMEM((tiles, LANES), F32),
                pltpu.VMEM(corners.shape, corners.dtype),
                pltpu.SemaphoreType.DMA((3,)),
                pltpu.VMEM((own_rows + 16, LANES), F32),
                pltpu.VMEM((tiles, LANES), F32),
                pltpu.VMEM((tiles, LANES), F32),
                pltpu.VMEM((LANES, LANES), F32),
                pltpu.VMEM((9, tiles, LANES), F32),
                pltpu.VMEM((3, tiles, LANES), F32),
                pltpu.VMEM((LANES, LANES), jnp.int32),
                pltpu.VMEM((3, tiles, LANES), jnp.int32),
                pltpu.VMEM((far_rows, LANES), F32),
                pltpu.VMEM((own_rows + 16, LANES), F32),
                pltpu.VMEM((1,) + row, F32),
                pltpu.VMEM((blocks,) + row, F32),
                pltpu.VMEM((sub_count,) + row, F32),
                pltpu.VMEM((blocks,) + row, F32),
                pltpu.VMEM((sub_count,) + row, F32),
                pltpu.VMEM((blocks,) + row, F32),
                pltpu.VMEM((sub_count,) + row, F32),
                pltpu.VMEM((blocks,) + row, F32),
                pltpu.SemaphoreType.DMA((2, sub_count)),
                pltpu.SemaphoreType.DMA((2, blocks)),
                pltpu.SemaphoreType.DMA((2, sub_count)),
                pltpu.SemaphoreType.DMA((2, blocks)),
            ],
            compiler_params=pltpu.CompilerParams(collective_id=0, has_side_effects=True),
            name="divergence",
        )(
            heat.reshape(own_rows, LANES),
            lists,
            live_faces,
            basis,
            area.reshape(tiles, LANES),
            corners,
        )
        return out.reshape(owned)

    placed = (
        P(("patch", "sub")),
        P(None, ("patch", "sub")),
        P(("patch", "sub")),
        P(None, ("patch", "sub")),
        P(("patch", "sub")),
        P(None, ("patch", "sub")),
        P(("patch", "sub")),
    )
    return jax.shard_map(
        per_device, mesh=mesh, in_specs=placed, out_specs=P(("patch", "sub")), check_vma=False
    )
```

time: 183 us -> 26.7 us (0.15)
  matrix products: 102 us -> 0 us
  other arithmetic: 43.4 us -> 0.6 us
  Pallas kernels: 0 us -> 23.1 us
  starting transfers between devices: 12.3 us -> 0 us
  blocking collectives: 11.5 us -> 0 us
  local copies, waits for them, and re-layouts: 9.11 us -> 2.04 us
  loops' own time: 1.96 us -> 0 us
    dot_general x64 -> x0, matrix products: 102 us -> none  [the longest x16 27.1 us: tile_terms(): jnp.einsum('kfw,w->kf', onehot_far, remote_window, precision=lax.Precisio...]
    pallas_call x0 -> x1, Pallas kernels: none -> 23.1 us  [per_device(): pl.pallas_call(functools.partial(kernel, patch_count, sub_count, share),...]
    select_n x19 -> x0, other arithmetic: 22.5 us -> none  [the longest x16 22.5 us: tile_terms(): weight = jnp.where(live_mask, area_tile, 0.0)]
    sub x16 -> x0, other arithmetic: 12.8 us -> none  [tile_terms(): corner_tile[:, :, None] - remote_start == remote_pos]
    ppermute x8 -> x0, starting transfers between devices: 12.3 us -> none  [from_behind(): lax.ppermute(x, axis, [(i, (i + by) % length) for i in range(length)])]
    unnamed x1 -> x0, blocking collectives: 6.48 us -> none
    scatter-add x2 -> x0, other arithmetic: 5.62 us -> none  [the longest x1 4.35 us: per_device(): result = result.at[send_pat.reshape(-1)].add(returned.reshape(-1))]
    all_gather x1 -> x0, blocking collectives: 5.06 us -> none  [per_device(): group_values = lax.all_gather(group_send, 'sub', axis=0, tiled=True)]
  transfers between devices with their start and end apart: 8 -> 0, of which waited for: 0 -> 0; matrix products, arithmetic and copies ran while one was open for 3% -> 0% of each run, Pallas kernels for 0% -> 0%
where the time goes in v1:
time: 26.7 us; the launch traced here: 26.4 us
  Pallas kernels  23.1 us (87%)
  local copies, waits for them, and re-layouts  2.04 us (8%)
  between operations  0.68 us (3%)
  other arithmetic  0.6 us (2%)
    pallas_call x1, Pallas kernels, per_device(): pl.pallas_call(functools.partial(kernel, patch_count, sub_count, share),...  23.1 us
    unnamed x5, local copies, waits for them, and re-layouts  2.04 us
    concatenate x1, other arithmetic, per_device(): jnp.concatenate([jnp.pad(send_sub, (0, LANES - share))[None], send_pat],...  0.6 us

profile of v1, /device:TPU:0, one launch (start us, length us, event | category | flops | bytes accessed | tf_op | source)
XLA Modules:
  0.0 26.4 jit_solution(10988166251361326599)
XLA Ops:
  0.7 0.0 copy-start
  0.7 0.0 copy-start.1
  0.7 0.7 %copy-done = s32[4,128]{1,0:T(4,128)S(1)} copy-done((s32[4,128]{1,0:T(4,128)S(1)}, s32[4,128]{1,0:T(4,128)}, u32[]{:S(2)}) %copy-start) | copy-done | bytes 2072
  1.3 0.0 copy-done.1
  1.3 0.6 %pad_add_fusion.sends_ref = s32[5,128]{1,0:T(8,128)} fusion(s32[4,128]{1,0:T(4,128)S(1)} %copy-done, s32[1,128]{1,0:T(1,128)S(1)} %bitcast.7), kind=kLoop, calls=%fused_computation | loop fusion | flops 640 | bytes 5120 | tf_op jit(solution)/shard_map/concatenate | solution.py:387
  1.9 23.1 %divergence.1 = f32[64,128]{1,0:T(8,128)} custom-call(f32[64,128]{1,0:T(8,128)} %bitcast.6, s32[5,128]{1,0:T(8,128)} %pad_add_fusion.sends_ref, s32[1]{0:T(128)S(6)} %copy.9.live_ref, bf16[9,16384]{1,0:T(8,128)(2,1)} %basis_hbm.1, f32[128,128]{1,0:T(8,128)} %bitcast.5, s32[3,16384]{1,0:T(4,128)} %corners_hbm.1), custom_call_target="tpu_custom_call" | custom-call | tf_op jit(solution)/shard_map/divergence/pallas_call | solution.py:391
  25.0 1.4 %copy.10 = f32[8192]{0:T(1024)} copy(f32[8192]{0:T(1024)} %bitcast.4) | data formatting | bytes 65536
Async XLA Ops:
  0.7 0.7 %copy-start = (s32[4,128]{1,0:T(4,128)S(1)}, s32[4,128]{1,0:T(4,128)}, u32[]{:S(2)}) copy-start(s32[4,128]{1,0:T(4,128)} %param.12) | copy-start | bytes 6148
  0.7 0.7 %copy-start.1 = (s32[128]{0:T(128)S(1)}, s32[128]{0:T(128)}, u32[]{:S(2)}) copy-start(s32[128]{0:T(128)} %param.11) | copy-start | bytes 1540

commit v2 on v1

--- a/solution.py
+++ b/solution.py
@@ -9,6 +9,7 @@
 
 RADIUS = 2
 LANES = 128
+HALF = 64
 F32 = jnp.float32
 BF16 = jnp.bfloat16
 
@@ -38,13 +39,18 @@
     patch_count,
     sub_count,
     share,
-    heat_ref,
-    sends_ref,
-    live_ref,
+    heat_hbm,
+    sub_list_hbm,
+    patch_list_hbm,
+    live_hbm,
     basis_hbm,
     area_hbm,
     corners_hbm,
     out_ref,
+    heat_ref,
+    sub_list_ref,
+    patch_list_ref,
+    live_ref,
     basis_in,
     area_in,
     corners_in,
@@ -57,7 +63,11 @@
     near_val,
     spot,
     parts,
+    terms,
+    hot_mem,
+    row_mem,
     far,
+    far_sum,
     near_sum,
     send_group,
     send_patch,
@@ -83,14 +93,6 @@
     per_row = LANES // share
     group_rows = sub_count // per_row
 
-    copies = [
-        pltpu.make_async_copy(corners_hbm, corners_in, in_sem.at[0]),
-        pltpu.make_async_copy(basis_hbm, basis_in, in_sem.at[1]),
-        pltpu.make_async_copy(area_hbm, area_in, in_sem.at[2]),
-    ]
-    for copy in copies:
-        copy.start()
-
     subs = [lax.rem(s + d, sub_count) for d in range(1, sub_count)]
     behind = [lax.rem(s + sub_count - d, sub_count) for d in range(1, sub_count)]
     ahead_patch = [lax.rem(p + o + patch_count, patch_count) for o in offsets]
@@ -101,11 +103,30 @@
     for target in ahead_patch:
         pl.semaphore_signal(barrier, inc=1, device_id={"patch": target, "sub": s})
 
+    early = [
+        pltpu.make_async_copy(heat_hbm, heat_ref, in_sem.at[0]),
+        pltpu.make_async_copy(sub_list_hbm, sub_list_ref, in_sem.at[1]),
+        pltpu.make_async_copy(patch_list_hbm, patch_list_ref, in_sem.at[2]),
+    ]
+    copies = [
+        pltpu.make_async_copy(corners_hbm, corners_in, in_sem.at[3]),
+        pltpu.make_async_copy(basis_hbm, basis_in, in_sem.at[4]),
+        pltpu.make_async_copy(area_hbm, area_in, in_sem.at[5]),
+        pltpu.make_async_copy(live_hbm, live_ref, in_sem.at[6]),
+    ]
+    for copy in early + copies:
+        copy.start()
+
+    for copy in early:
+        copy.wait()
     heat = heat_ref[...]
     piece_a, rest = split_two(heat)
     piece_b, piece_c = split_two(rest)
     pieces = jnp.concatenate([piece_a, piece_b, piece_c], axis=0).astype(BF16)
-    lists = sends_ref[...]
+    sub_list = sub_list_ref[...]
+    if share < LANES:
+        sub_list = jnp.concatenate([sub_list, jnp.zeros((1, LANES - share), jnp.int32)], axis=1)
+    lists = jnp.concatenate([sub_list, patch_list_ref[...]], axis=0)
     rows_of = lax.shift_right_logical(lists, 7).astype(F32)
     lanes_of = (lists & (LANES - 1)).astype(F32)
     row_iota = lax.broadcasted_iota(jnp.int32, (own_rows, LANES), 0).astype(F32)
@@ -177,6 +198,8 @@
 
     for copy in copies:
         copy.wait()
+    one = jnp.ones((16, LANES), BF16)
+    zero = jnp.zeros((16, LANES), BF16)
     sub8 = lax.broadcasted_iota(jnp.int32, (8, LANES), 0)
 
     def prepare(g, carry):
@@ -201,6 +224,32 @@
         return carry
 
     lax.fori_loop(0, groups, prepare, 0)
+
+    id_iota = lax.broadcasted_iota(jnp.int32, (32, LANES), 0).astype(F32).astype(BF16)
+    hot_iota = lane_iota[:HALF].astype(BF16)
+
+    def encode(g, carry):
+        tile = pl.ds(pl.multiple_of(8 * g, 8), 8)
+        for k in range(3):
+            pos = parts[k, tile, :]
+            lanes = (pos & (HALF - 1)).astype(F32)
+            rows = lax.shift_right_logical(pos, 6)
+            ids = jnp.where(
+                rows >= 2 * own_rows, rows - 2 * own_rows, rows - 8 * g + 2 + 2 * far_rows
+            ).astype(F32)
+            for i in range(8):
+                cols = slice((3 * i + k) * LANES, (3 * i + k + 1) * LANES)
+                lane_wide = wide(lanes[i : i + 1], 16).astype(BF16)
+                for n in range(HALF // 16):
+                    part = slice(16 * n, 16 * n + 16)
+                    hot_mem[g, part, cols] = jnp.where(lane_wide == hot_iota[part], one, zero)
+                id_wide = wide(ids[i : i + 1], 16).astype(BF16)
+                for n in range(2):
+                    part = slice(16 * n, 16 * n + 16)
+                    row_mem[g, part, cols] = jnp.where(id_wide == id_iota[part], one, zero)
+        return carry
+
+    lax.fori_loop(0, groups, encode, 0)
 
     for d, source in enumerate(behind):
         to_sub(
@@ -235,69 +284,62 @@
     odd = jnp.concatenate([far[pl.ds(1, windows, stride=2), :]] * (8 // windows), axis=0)
     live = live_ref[0]
     lane_ids = lax.broadcasted_iota(jnp.int32, (8, LANES), 1)
-    id_iota = lax.broadcasted_iota(jnp.int32, (16, LANES), 0).astype(F32).astype(BF16)
-    hot_iota = lane_iota.astype(BF16)
-    one = jnp.ones((16, LANES), BF16)
-    zero = jnp.zeros((16, LANES), BF16)
     near_sum[...] = jnp.zeros_like(near_sum)
 
-    def work(g, far_acc):
+    def evaluate(g, carry):
         first = pl.multiple_of(8 * g, 8)
         tile = pl.ds(first, 8)
-        values, lanes, ids = [], [], []
+        values = []
         for k in range(3):
             pos = parts[k, tile, :]
             lane = pos & (LANES - 1)
             row = lax.shift_right_logical(pos, 7)
             remote = jnp.where((row & 1) == 0, lane_pick(even, lane), lane_pick(odd, lane))
             values.append(jnp.where(row >= own_rows, remote, near_val[k, tile, :]))
-            lanes.append(lane.astype(F32))
-            ids.append(
-                jnp.where(row >= own_rows, row - own_rows, row - 4 * g + 1 + far_rows).astype(F32)
-            )
         grad = [[grads[3 * k + c, tile, :] for c in range(3)] for k in range(3)]
         total = [sum(grad[k][c] * values[k] for k in range(3)) for c in range(3)]
         squared = total[0] * total[0] + total[1] * total[1] + total[2] * total[2]
         scale = -1.0 / jnp.maximum(jnp.sqrt(squared), 1.0)
         slot = (first + sub8) * LANES + lane_ids
         scale = scale * jnp.where(slot < live, area_in[tile, :], 0.0)
-        tops, lows = [], []
         for k in range(3):
             term = (
                 grad[k][0] * total[0] + grad[k][1] * total[1] + grad[k][2] * total[2]
             ) * scale
             high, low = split_two(term)
-            tops.append(high)
-            lows.append(low)
-        acc = jnp.zeros((32, LANES), F32)
-        for pair in range(4):
-            left, right = [], []
-            for i in (2 * pair, 2 * pair + 1):
-                for k in range(3):
-                    id_wide = wide(ids[k][i : i + 1], 16).astype(BF16)
-                    top = wide(tops[k][i : i + 1], 16).astype(BF16)
-                    low = wide(lows[k][i : i + 1], 16).astype(BF16)
-                    mask = id_wide == id_iota
-                    left.append(
-                        jnp.concatenate([jnp.where(mask, top, zero), jnp.where(mask, low, zero)], axis=0)
-                    )
-                    lane_wide = wide(lanes[k][i : i + 1], 16).astype(BF16)
-                    right.append(
-                        jnp.concatenate(
-                            [
-                                jnp.where(lane_wide == hot_iota[16 * n : 16 * n + 16], one, zero)
-                                for n in range(LANES // 16)
-                            ],
-                            axis=0,
-                        )
-                    )
-            acc = acc + rows_dot(jnp.concatenate(left, axis=1), jnp.concatenate(right, axis=1))
-        acc = acc[:16] + acc[16:]
-        at = pl.ds(pl.multiple_of(4 * g, 4), 8)
-        near_sum[at, :] = near_sum[at, :] + acc[8:]
-        return far_acc + acc[:8]
-
-    sums = lax.fori_loop(0, groups, work, jnp.zeros((8, LANES), F32))
+            terms[k, tile, :] = high
+            terms[3 + k, tile, :] = low
+        return carry
+
+    lax.fori_loop(0, groups, evaluate, 0, unroll=4)
+
+    def scatter(g, far_acc):
+        first = pl.multiple_of(8 * g, 8)
+        tile = pl.ds(first, 8)
+        rows = [terms[k, tile, :] for k in range(6)]
+        left = []
+        for i in range(8):
+            for k in range(3):
+                cols = slice((3 * i + k) * LANES, (3 * i + k + 1) * LANES)
+                top = wide(rows[k][i : i + 1], 16).astype(BF16)
+                low = wide(rows[3 + k][i : i + 1], 16).astype(BF16)
+                up, down = row_mem[g, :16, cols], row_mem[g, 16:, cols]
+                left.append(
+                    jnp.concatenate([up * top, down * top, up * low, down * low], axis=0)
+                )
+        acc = rows_dot(jnp.concatenate(left, axis=1), hot_mem[g])
+        acc = acc[:32] + acc[32:]
+        at = pl.ds(first, 16)
+        near_sum[at, :HALF] = near_sum[at, :HALF] + acc[16:]
+        return far_acc + acc[:16]
+
+    far_sum[:, :HALF] = lax.fori_loop(0, groups, scatter, jnp.zeros((16, HALF), F32), unroll=4)
+    lane8s = lax.broadcasted_iota(jnp.int32, (far_rows, LANES), 1)
+    sums = jnp.where(
+        lane8s < HALF,
+        far_sum[pl.ds(0, far_rows, stride=2), :],
+        pltpu.roll(far_sum[pl.ds(1, far_rows, stride=2), :], HALF, 1),
+    )
 
     for target in range(sub_count):
         row = sums[target // per_row : target // per_row + 1]
@@ -335,6 +377,11 @@
         hot.append(jnp.where(lane_wide == lane_iota, 1.0, 0.0).astype(BF16))
     hot = jnp.concatenate(hot, axis=1)
 
+    near = jnp.where(
+        lane8 < HALF,
+        near_sum[pl.ds(2, own_rows, stride=2), :],
+        pltpu.roll(near_sum[pl.ds(3, own_rows, stride=2), :], HALF, 1),
+    )
     for d, source in enumerate(behind):
         to_sub(
             back_group.at[source],
@@ -369,7 +416,7 @@
             ).astype(BF16)
         )
     added = rows_dot(jnp.concatenate(left, axis=1), hot)
-    out_ref[...] = near_sum[1 : 1 + own_rows, :] + added[:own_rows] + added[own_rows:]
+    out_ref[...] = near + added[:own_rows] + added[own_rows:]
     for copy in sent:
         copy.wait_send()
 
@@ -384,20 +431,23 @@
         own_rows, tiles = owned // LANES, slots // LANES
         far_rows = (sub_count * share + blocks * block_size) // LANES
         assert block_size == LANES and LANES % share == 0 and far_rows == 8
-        lists = jnp.concatenate([jnp.pad(send_sub, (0, LANES - share))[None], send_pat], axis=0)
         vmem = pl.BlockSpec(memory_space=pltpu.VMEM)
         hbm = pl.BlockSpec(memory_space=pl.ANY)
         row = (1, LANES)
         out = pl.pallas_call(
             functools.partial(kernel, patch_count, sub_count, share),
-            out_shape=jax.ShapeDtypeStruct((own_rows, LANES), F32),
-            in_specs=[vmem, vmem, pl.BlockSpec(memory_space=pltpu.SMEM), hbm, hbm, hbm],
+            out_shape=pltpu.VMEM((own_rows, LANES), F32),
+            in_specs=[hbm] * 7,
             out_specs=vmem,
             scratch_shapes=[
+                pltpu.VMEM((own_rows, LANES), F32),
+                pltpu.VMEM((1, share), jnp.int32),
+                pltpu.VMEM(send_pat.shape, jnp.int32),
+                pltpu.SMEM((1,), jnp.int32),
                 pltpu.VMEM(basis.shape, basis.dtype),
                 pltpu.VMEM((tiles, LANES), F32),
                 pltpu.VMEM(corners.shape, corners.dtype),
-                pltpu.SemaphoreType.DMA((3,)),
+                pltpu.SemaphoreType.DMA((7,)),
                 pltpu.VMEM((own_rows + 16, LANES), F32),
                 pltpu.VMEM((tiles, LANES), F32),
                 pltpu.VMEM((tiles, LANES), F32),
@@ -406,8 +456,12 @@
                 pltpu.VMEM((3, tiles, LANES), F32),
                 pltpu.VMEM((LANES, LANES), jnp.int32),
                 pltpu.VMEM((3, tiles, LANES), jnp.int32),
+                pltpu.VMEM((6, tiles, LANES), F32),
+                pltpu.VMEM((tiles // 8, HALF, 24 * LANES), BF16),
+                pltpu.VMEM((tiles // 8, 32, 24 * LANES), BF16),
                 pltpu.VMEM((far_rows, LANES), F32),
-                pltpu.VMEM((own_rows + 16, LANES), F32),
+                pltpu.VMEM((2 * far_rows, LANES), F32),
+                pltpu.VMEM((2 * own_rows + 16, LANES), F32),
                 pltpu.VMEM((1,) + row, F32),
                 pltpu.VMEM((blocks,) + row, F32),
                 pltpu.VMEM((sub_count,) + row, F32),
@@ -425,7 +479,8 @@
             name="divergence",
         )(
             heat.reshape(own_rows, LANES),
-            lists,
+            send_sub.reshape(1, share),
+            send_pat,
             live_faces,
             basis,
             area.reshape(tiles, LANES),

time: 26.7 us -> 18.9 us (0.71)
  Pallas kernels: 23.1 us -> 17.5 us
  local copies, waits for them, and re-layouts: 2.04 us -> 0.62 us
  other arithmetic: 0.6 us -> 0 us
    pallas_call x1, Pallas kernels: 23.1 us -> 17.5 us  [per_device(): pl.pallas_call(functools.partial(kernel, patch_count, sub_count, share),...]
    unnamed x5 -> x1, local copies, waits for them, and re-layouts: 2.04 us -> 0.62 us
    concatenate x1 -> x0, other arithmetic: 0.6 us -> none  [per_device(): jnp.concatenate([jnp.pad(send_sub, (0, LANES - share))[None], send_pat],...]
where the time goes in v2:
time: 18.9 us; the launch traced here: 18.7 us
  Pallas kernels  17.5 us (93%)
  between operations  0.66 us (3%)
  local copies, waits for them, and re-layouts  0.62 us (3%)
    pallas_call x1, Pallas kernels, per_device(): pl.pallas_call(functools.partial(kernel, patch_count, sub_count, share),...  17.5 us
    unnamed x1, local copies, waits for them, and re-layouts  0.62 us

profile of v2, /device:TPU:0, one launch (start us, length us, event | category | flops | bytes accessed | tf_op | source)
XLA Modules:
  0.0 18.7 jit_solution(16906232915714226463)
XLA Ops:
  0.7 17.5 %divergence.1 = f32[64,128]{1,0:T(8,128)S(1)} custom-call(f32[64,128]{1,0:T(8,128)} %bitcast.6, s32[1,128]{1,0:T(1,128)} %bitcast.7, s32[4,128]{1,0:T(4,128)} %patch_list_hbm.1, s32[1]{0:T(128)S(6)} %copy.10.live_hbm, bf16[9,16384]{1,0:T(8,128)(2,1)} %basis_hbm.1, f32[128,128]{1,0:T(8,128)} %bitcast.5, s32[3,16384]{1,0:T(4,128)} %corners_hbm.1), custom_call_target="tpu_custom_call" | custom-call | tf_op jit(solution)/shard_map/divergence/pallas_call | solution.py:437
  18.1 0.6 %copy.9 = f32[8192]{0:T(1024)} copy(f32[8192]{0:T(1024)S(1)} %bitcast.4) | data formatting | bytes 65536
